TPU v7x, 256 devices: a whole 4x4x8 slice. The times are simulated.
256 devices in a mesh: fsdp: 16 (over y, x), width: 16 (over z, core).
Axes of the slice: x: 4, y: 4, z: 8, core: 2. Of those that a mesh axis runs over, the one named last changes fastest.
Arguments:
- train_gate: float32 [4096, 11008], P('fsdp', 'width'), may hold values from -0.125 to 0.125
- drift_gate: float32 [4096, 11008], P('fsdp', 'width'), may hold values from -0.09375 to 0.09375
- spread_gate: float32 [4096, 11008], P('fsdp', 'width'), may hold values from -0.09375 to 0.09375
- train_up: float32 [4096, 11008], P('fsdp', 'width'), may hold values from -0.125 to 0.125
- drift_up: float32 [4096, 11008], P('fsdp', 'width'), may hold values from -0.09375 to 0.09375
- spread_up: float32 [4096, 11008], P('fsdp', 'width'), may hold values from -0.09375 to 0.09375
- norm_train: float32 [4096], P(('fsdp', 'width')), may hold values from 0.25 to 1.75
- norm_step: float32 [4096], P(('fsdp', 'width')), may hold values from -0.3 to 0.3
Outputs:
- serving_gate: bfloat16 [4096, 11008], P(None, 'width')
- serving_up: bfloat16 [4096, 11008], P(None, 'width')
- scale_gate: float32 [11008], P('width')
- scale_up: float32 [11008], P('width')
- serve_norm: bfloat16 [4096], replicated
- whole_gate: float32 [4096, 11008], P('fsdp', 'width')
- whole_up: float32 [4096, 11008], P('fsdp', 'width')
All inputs are finite; a program needn't handle non-finite values.
Results may differ from a plain program's by a relative error of at most 0.0004.
Values may be sent and summed in bfloat16 or wider, within the bound.
A program may use at most 128 MiB of HBM per device.

v0:
```python
import jax
import jax.numpy as jnp
from jax import lax
from jax.sharding import Mesh
from jax.sharding import PartitionSpec as P

FSDP = ("fsdp_0", "fsdp_1")
FSDP_WIDTH = ("fsdp_0", "fsdp_1", "width")


learn_rate = 0.3
hold_rate = 0.9


def one_axis_at_a_time(array, axes):
    for axis in axes:
        array = lax.psum(array, axis)
    return array


def side_by_side(arrays, axis, dim, along):
    both = jnp.concatenate(arrays, axis=along)
    result, at, done = (lax.all_gather(both, axis, axis=dim, tiled=True), 0, [])
    for a in arrays:
        done.append(lax.slice_in_dim(result, at, at + a.shape[along], axis=along))
        at += a.shape[along]
    return tuple(done)


def shards(
    train_gate, drift_gate, spread_gate, train_up, drift_up, spread_up, norm_train, norm_step
):
    hold_gate = hold_rate * drift_gate + spread_gate
    whole_gate = train_gate - learn_rate * hold_gate
    hold_up = hold_rate * drift_up + spread_up
    whole_up = train_up - learn_rate * hold_up
    total_gate, total_up = (
        one_axis_at_a_time(jnp.sum(whole_gate * whole_gate, axis=0), FSDP),
        one_axis_at_a_time(jnp.sum(whole_up * whole_up, axis=0), FSDP),
    )
    scale_gate = jnp.sqrt(total_gate)
    scale_up = jnp.sqrt(total_up)
    narrow_gate, narrow_up = (
        (whole_gate / scale_gate).astype(jnp.bfloat16),
        (whole_up / scale_up).astype(jnp.bfloat16),
    )
    serving_gate, serving_up = side_by_side((narrow_gate, narrow_up), FSDP, 0, 1)
    serve_norm = lax.all_gather(
        (norm_train + norm_step).astype(jnp.bfloat16), FSDP_WIDTH, axis=0, tiled=True
    )
    return (serving_gate, serving_up, scale_gate, scale_up, serve_norm, whole_gate, whole_up)


def solution(mesh):
    split = Mesh(mesh.devices.reshape(4, 4, mesh.shape["width"]), ("fsdp_0", "fsdp_1", "width"))
    in_specs = (
        P(FSDP, "width"),
        P(FSDP, "width"),
        P(FSDP, "width"),
        P(FSDP, "width"),
        P(FSDP, "width"),
        P(FSDP, "width"),
        P(FSDP_WIDTH),
        P(FSDP_WIDTH),
    )
    out_specs = (
        P(None, "width"),
        P(None, "width"),
        P("width"),
        P("width"),
        P(),
        P(FSDP, "width"),
        P(FSDP, "width"),
    )
    return jax.shard_map(
        shards, mesh=split, in_specs=in_specs, out_specs=out_specs, check_vma=False
    )
```

profile of v0, /device:TPU:2, one launch (start us, length us, event | category | flops | bytes accessed | tf_op | source)
XLA Modules:
  0.0 145.8 jit_solution(3862906683493786616)
XLA Ops:
  7.2 0.0 copy-start.4
  7.2 0.0 copy-start.5
  7.2 0.0 all-gather.2.cloned.1.call-start
  7.2 2.5 %multiply_reduce_fusion = (f32[688]{0:T(1024)S(1)}, f32[256,688]{0,1:T(8,128)S(1)}, f32[688]{0:T(1024)S(1)}, f32[256,688]{0,1:T(8,128)S(1)}) fusion(f32[256,688]{0,1:T(8,128)} %param.11, f32[256,688]{0,1:T(8,128)} %param.13, f32[256,688]{0,1:T(8,128)} %param.12, f32[256,688]{0,1:T(8,128)} %param.8, f32[256,688]{0,1:T(8,128)} %param.10, f32[256,688]{0,1:T(8,128)} %param.9), kind=kLoop, calls=%fused_computation.2 | loop fusion | flops 2112160 | bytes 5641600 | tf_op jit(solution)/shard_map/reduce_sum | solution.py:39
  9.8 0.0 copy-start
  9.8 0.0 copy-start.1
  9.8 10.9 %all-reduce.2 = (f32[688]{0:T(1024)S(1)}, f32[688]{0:T(1024)S(1)}) all-reduce(f32[688]{0:T(1024)S(1)} %get-tuple-element.13, f32[688]{0:T(1024)S(1)} %get-tuple-element.17), channel_id=1, replica_groups=mesh['fsdp_0'=4,'fsdp_1'=4,'width'=16] {'fsdp_0'}, use_global_device_ids=true, to_apply=%region_4.0 | all-reduce | flops 1376 | bytes 11008 | tf_op jit(solution)/shard_map/psum | solution.py:17
  20.7 8.8 %all-reduce.1 = (f32[688]{0:T(1024)S(1)}, f32[688]{0:T(1024)S(1)}) all-reduce(f32[688]{0:T(1024)S(1)} %get-tuple-element.9, f32[688]{0:T(1024)S(1)} %get-tuple-element.10), channel_id=1, replica_groups=mesh['fsdp_0'=4,'fsdp_1'=4,'width'=16] {'fsdp_1'}, use_global_device_ids=true, to_apply=%region_5.0 | all-reduce | flops 1376 | bytes 11008 | tf_op jit(solution)/shard_map/psum | solution.py:17
  29.5 0.0 copy-start.2
  29.5 0.0 copy-start.3
  29.5 0.2 divide_convert_fusion.1
  29.7 0.2 divide_convert_fusion
  29.9 0.9 pad_maximum_fusion
  30.8 0.0 all-gather.2.cloned.1.call-update
  30.8 0.0 copy-done.4
  30.8 0.0 copy-done.5
  30.8 0.2 dynamic-update-slice
  31.1 80.0 %all-reduce = bf16[4096]{0:T(1024)(128)(2,1)} all-reduce(bf16[4096]{0:T(1024)(128)(2,1)S(1)} %dynamic-update-slice), channel_id=1, replica_groups=mesh['fsdp_0'=4,'fsdp_1'=4,'width'=16] {'fsdp_0','fsdp_1','width'}, use_global_device_ids=true, to_apply=%add | all-reduce | flops 4096 | bytes 16384
  111.0 17.4 %all-gather.2.cloned.1.call-done = bf16[4096,1376]{0,1:T(8,128)(2,1)} async-done(((bf16[256,1376]{0,1:T(8,128)(2,1)}), bf16[4096,1376]{0,1:T(8,128)(2,1)}) %all-gather.2.cloned.1.call-update) | async-done | bytes 11272208 | tf_op jit(solution)/shard_map/all_gather | solution.py:23
  128.5 10.5 %fusion = (bf16[4096,688]{0,1:T(8,128)(2,1)}, bf16[4096,688]{0,1:T(8,128)(2,1)}) fusion(bf16[4096,1376]{0,1:T(8,128)(2,1)} %all-gather.2.cloned.1.call-done), kind=kLoop, calls=%fused_computation.8 | loop fusion | bytes 22544384 | tf_op jit(solution)/shard_map/slice | solution.py:25
  138.9 0.0 copy-done
  138.9 0.0 copy-done.1
  138.9 0.0 copy-done.2
  138.9 0.0 copy-done.3
  (4 shorter events, 0.0 us)
Async XLA Ops:
  7.2 23.6 %copy-start.4 = (f32[16]{0:T(128)S(1)}, f32[16]{0:T(128)}, u32[]{:S(2)}) copy-start(f32[16]{0:T(128)} %param.14) | copy-start | bytes 196
  7.2 23.6 %copy-start.5 = (f32[16]{0:T(128)S(1)}, f32[16]{0:T(128)}, u32[]{:S(2)}) copy-start(f32[16]{0:T(128)} %param.15) | copy-start | bytes 196
  7.2 121.3 %all-gather.2.cloned.1.call-start = ((), (), s32[]{:S(2)}) async-start(), calls=%async_computation | async-start | bytes 11976704 | tf_op jit(solution)/shard_map/all_gather | solution.py:23
  9.8 129.2 %copy-start = (f32[256,688]{0,1:T(8,128)}, f32[256,688]{0,1:T(8,128)S(1)}, u32[]{:S(2)}) copy-start(f32[256,688]{0,1:T(8,128)S(1)} %get-tuple-element.14) | copy-start | bytes 2113540
  9.8 129.2 %copy-start.1 = (f32[256,688]{0,1:T(8,128)}, f32[256,688]{0,1:T(8,128)S(1)}, u32[]{:S(2)}) copy-start(f32[256,688]{0,1:T(8,128)S(1)} %get-tuple-element.18) | copy-start | bytes 2113540
  29.5 109.4 %copy-start.2 = (f32[688]{0:T(1024)}, f32[688]{0:T(1024)S(1)}, u32[]{:S(2)}) copy-start(f32[688]{0:T(1024)S(1)} %sqrt.6) | copy-start | bytes 8260
  29.5 109.4 %copy-start.3 = (f32[688]{0:T(1024)}, f32[688]{0:T(1024)S(1)}, u32[]{:S(2)}) copy-start(f32[688]{0:T(1024)S(1)} %sqrt.7) | copy-start | bytes 8260
Sparse Core Ops, SparseCore 0:
  30.9 97.5 all-gather.1
where the time goes:
time: 146 us
  blocking collectives  99.6 us (68%)
  waiting for transfers between devices  17.4 us (12%)
  between operations  14.2 us (10%)
  local copies, waits for them, and re-layouts  10.8 us (7%)
  other arithmetic  3.76 us (3%)
    unnamed x1, blocking collectives  80 us
    psum x2, blocking collectives, one_axis_at_a_time(): array = lax.psum(array, axis)  19.7 us
    all_gather x1, waiting for transfers between devices, side_by_side(): result, at, done = (lax.all_gather(both, axis, axis=dim, tiled=True), 0, [])  17.4 us
    slice x1, local copies, waits for them, and re-layouts, side_by_side(): done.append(lax.slice_in_dim(result, at, at + a.shape[along], axis=along))  10.5 us
  transfers between devices with their start and end apart: 1, of which 1 were waited for; matrix products, arithmetic and copies ran while one was open for 0% of the time, Pallas kernels for 0%

commit v1 on v0

v1 whole, which is shorter than its diff:
```python
import functools

import jax
import jax.numpy as jnp
from jax import lax
from jax.experimental import pallas as pl
from jax.experimental.pallas import tpu as pltpu
from jax.sharding import Mesh
from jax.sharding import PartitionSpec as P

FSDP = ("fsdp_0", "fsdp_1")
FSDP_WIDTH = ("fsdp_0", "fsdp_1", "width")
RING = 4
LANES = 128
NORM_ROW = 14

learn_rate = 0.3
hold_rate = 0.9


def chunks(columns):
    return [(at, min(LANES, columns - at)) for at in range(0, columns, LANES)]


def kernel(n_width, tg, dg, sg, tu, du, su, norm,
           og, ou, scale_g, scale_u, serve, wg, wu,
           held, sums, parts, ordered,
           in_sems, sum_send, sum_recv, part_send, part_recv, send_sems, recv_sems):
    y, x, w = lax.axis_index("fsdp_0"), lax.axis_index("fsdp_1"), lax.axis_index("width")
    me = y * RING + x
    columns, rows = wg.shape

    def at(yy, xx, ww):
        return {"device_id": (yy, xx, ww), "device_id_type": pl.DeviceIdType.MESH}

    loads = [pltpu.make_async_copy(ref, held.at[i], in_sems.at[i])
             for i, ref in enumerate((tg, dg, sg, tu, du, su))]
    for load in loads:
        load.start()

    plane = sorted(((dy, dx) for dy in range(RING) for dx in range(RING) if dy or dx),
                   key=lambda d: -(min(d[0], RING - d[0]) + min(d[1], RING - d[1])))
    mates = [((y + dy) % RING, (x + dx) % RING, w) for dy, dx in plane]
    stack = [(y, x, (w + dw) % n_width) for dw in range(1, n_width)]

    barrier = pltpu.get_barrier_semaphore()
    for peer in mates + stack:
        pl.semaphore_signal(barrier, 1, **at(*peer))

    sums[me] = jnp.zeros((16, LANES), jnp.float32)
    sums[me, NORM_ROW:NORM_ROW + 1, :] = norm[...]
    for a, whole in enumerate((wg, wu)):
        for load in loads[3 * a:3 * a + 3]:
            load.wait()
        for k, (start, size) in enumerate(chunks(columns)):
            part = pl.ds(start, size)
            hold = hold_rate * held[3 * a + 1, part, :] + held[3 * a + 2, part, :]
            new = held[3 * a, part, :] - learn_rate * hold
            whole[part, :] = new
            square = new * new
            folded = square[:, :LANES]
            for j in range(LANES, rows, LANES):
                folded = folded + square[:, j:j + LANES]
            if size < LANES:
                folded = jnp.concatenate([folded, jnp.zeros((LANES - size, LANES), jnp.float32)], axis=0)
            sums[me, 8 * a + k:8 * a + k + 1, :] = jnp.sum(folded.T, axis=0, keepdims=True)

    pl.semaphore_wait(barrier, len(mates) + len(stack))

    sent = []
    for i, peer in enumerate(mates):
        copy = pltpu.make_async_remote_copy(sums.at[me], sums.at[me], sum_send.at[i], sum_recv.at[i], **at(*peer))
        copy.start()
        sent.append(copy)
    for i, (dy, dx) in enumerate(plane):
        source = ((y + RING - dy) % RING) * RING + (x + RING - dx) % RING
        pltpu.make_async_remote_copy(sums.at[source], sums.at[source], sum_send.at[i], sum_recv.at[i],
                                     **at(*mates[i])).wait_recv()
    total = sums[0]
    for i in range(1, RING * RING):
        total = total + sums[i]
    scale = jnp.sqrt(total)
    inverse = jnp.concatenate([1.0 / scale, jnp.zeros((LANES - 16, LANES), jnp.float32)], axis=0).T
    own = pl.ds(pl.multiple_of(me * rows, LANES), rows)
    for a, (whole, out) in enumerate(((wg, og), (wu, ou))):
        for k, (start, size) in enumerate(chunks(columns)):
            part = pl.ds(start, size)
            factor = inverse[:size, 8 * a + k:8 * a + k + 1]
            out[part, own] = (whole[part, :] * factor).astype(jnp.bfloat16)
    scale_g[...] = scale[:8]
    scale_u[...] = scale[8:]
    for i in range(RING * RING):
        parts[w, i:i + 1, :] = sums[i, NORM_ROW:NORM_ROW + 1, :]

    half = columns // 2 // 8 * 8
    halves = {1: pl.ds(0, half), -1: pl.ds(half, columns - half)}
    full = pl.ds(0, columns)
    outs = (og, ou)
    keys = {}

    def block(a, p, q):
        p, q = (p + RING) % RING, (q + RING) % RING
        index = q * RING + p if a == 0 else p * RING + q
        return pl.ds(pl.multiple_of(index * rows, LANES), rows)

    def peer(a, phase, d):
        along_x = (a == 0) == (phase == 1)
        if along_x:
            return at(y, (x + d + RING) % RING, w)
        return at((y + d + RING) % RING, x, w)

    def copy_of(key, a, phase, d, part, cols):
        index = keys.setdefault(key, len(keys))
        ref = outs[a].at[part, cols]
        return pltpu.make_async_remote_copy(ref, ref, send_sems.at[index], recv_sems.at[index], **peer(a, phase, d))

    def send(key, a, phase, d, part, cols):
        copy = copy_of(key, a, phase, d, part, cols)
        copy.start()
        sent.append(copy)

    def receive(key, a, phase, d, part, cols):
        copy_of(key, a, phase, d, part, cols).wait_recv()

    spots = ((x, y), (y, x))
    both = [(a, d) for a in range(2) for d in (1, -1)]
    for a, d in both:
        p, q = spots[a]
        send(("first", a, d), a, 1, d, full, block(a, p, q))
    for a, d in both:
        p, q = spots[a]
        send(("second", a, 0, d), a, 2, d, full, block(a, p, q))
    for i, mate in enumerate(stack):
        copy = pltpu.make_async_remote_copy(parts.at[w], parts.at[w], part_send.at[i], part_recv.at[i], **at(*mate))
        copy.start()
        sent.append(copy)
    for a, d in both:
        p, q = spots[a]
        receive(("first", a, d), a, 1, d, full, block(a, p - d, q))
        send(("pass", a, d), a, 1, d, halves[d], block(a, p - d, q))
    for a, e in both:
        p, q = spots[a]
        for d in (1, -1):
            send(("second", a, e, d), a, 2, d, full, block(a, p - e, q))
    for a, e in both:
        p, q = spots[a]
        receive(("pass", a, e), a, 1, e, halves[e], block(a, p - 2 * e, q))
        for d in (1, -1):
            send(("second", a, 2 * e, d), a, 2, d, halves[e], block(a, p + 2, q))
    for e in (0, 1, -1):
        for a, d in both:
            p, q = spots[a]
            receive(("second", a, e, d), a, 2, d, full, block(a, p - e, q - d))
            send(("end", a, e, d), a, 2, d, halves[d], block(a, p - e, q - d))
    for a, d in both:
        p, q = spots[a]
        receive(("second", a, 2 * d, d), a, 2, d, halves[d], block(a, p + 2, q - d))
        send(("end", a, 2, d), a, 2, d, halves[d], block(a, p + 2, q - d))

    for i, (_, _, target) in enumerate(stack):
        source = (w + n_width - (i + 1)) % n_width
        pltpu.make_async_remote_copy(parts.at[source], parts.at[source], part_send.at[i], part_recv.at[i],
                                     **at(*stack[i])).wait_recv()
    strips = ordered.shape[0] // 16
    for b in range(strips):
        group = [parts[i] for i in range(b * n_width // strips, (b + 1) * n_width // strips)]
        ordered[pl.ds(b, 16, stride=strips), :] = functools.reduce(jnp.add, group)
    serve[...] = ordered[...].astype(jnp.bfloat16)

    for a, d in both:
        p, q = spots[a]
        receive(("second", a, -2 * d, d), a, 2, d, halves[-d], block(a, p + 2, q - d))
    for e in (0, 1, -1, 2):
        for a, d in both:
            p, q = spots[a]
            receive(("end", a, e, d), a, 2, d, halves[d], block(a, p - e, q - 2 * d))
    for copy in sent:
        copy.wait_send()


def shards(n_width, train_gate, drift_gate, spread_gate, train_up, drift_up, spread_up, norm_train, norm_step):
    rows, columns = train_gate.shape
    length = norm_train.shape[0]
    strips = n_width * length // LANES
    slot = lax.axis_index("width") * length % LANES // length
    lane = lax.broadcasted_iota(jnp.int32, (1, LANES), 1) // length
    norm = jnp.tile(norm_train + norm_step, LANES // length).reshape(1, LANES)
    norm = jnp.where(lane == slot, norm, 0.0)
    n_copies = 2 * 22
    VMEM, DMA = pltpu.VMEM, pltpu.SemaphoreType.DMA
    space = pl.BlockSpec(memory_space=pltpu.VMEM)
    og, ou, scale_g, scale_u, serve, wg, wu = pl.pallas_call(
        functools.partial(kernel, n_width),
        out_shape=[
            VMEM((columns, RING * RING * rows), jnp.bfloat16),
            VMEM((columns, RING * RING * rows), jnp.bfloat16),
            VMEM((8, LANES), jnp.float32),
            VMEM((8, LANES), jnp.float32),
            VMEM((16 * strips, LANES), jnp.bfloat16),
            VMEM((columns, rows), jnp.float32),
            VMEM((columns, rows), jnp.float32),
        ],
        in_specs=[pl.BlockSpec(memory_space=pltpu.HBM)] * 6 + [space],
        out_specs=[space] * 7,
        scratch_shapes=[
            VMEM((6, columns, rows), jnp.float32),
            VMEM((RING * RING, 16, LANES), jnp.float32),
            VMEM((n_width, 16, LANES), jnp.float32),
            VMEM((16 * strips, LANES), jnp.float32),
            DMA((6,)),
            DMA((RING * RING - 1,)),
            DMA((RING * RING - 1,)),
            DMA((n_width - 1,)),
            DMA((n_width - 1,)),
            DMA((n_copies,)),
            DMA((n_copies,)),
        ],
        compiler_params=pltpu.CompilerParams(collective_id=0, has_side_effects=True, vmem_limit_bytes=32 * 2**20),
    )(*(pltpu.with_memory_space_constraint(a.T, pltpu.HBM)
        for a in (train_gate, drift_gate, spread_gate, train_up, drift_up, spread_up)), norm)
    return (
        og.T, ou.T, scale_g.reshape(-1)[:columns], scale_u.reshape(-1)[:columns],
        serve.reshape(-1), wg.T, wu.T,
    )


def solution(mesh):
    split = Mesh(mesh.devices.reshape(RING, RING, mesh.shape["width"]), FSDP_WIDTH)
    weights = P(FSDP, "width")
    return jax.shard_map(
        functools.partial(shards, mesh.shape["width"]),
        mesh=split,
        in_specs=(weights,) * 6 + (P(FSDP_WIDTH),) * 2,
        out_specs=(P(None, "width"), P(None, "width"), P("width"), P("width"), P(), weights, weights),
        check_vma=False,
    )
```

time: 146 us -> 84.4 us (0.58)
  blocking collectives: 99.6 us -> 0 us
  Pallas kernels: 0 us -> 74.2 us
  waiting for transfers between devices: 17.4 us -> 0 us
  between operations: 14.2 us -> 0.68 us
  other arithmetic: 3.76 us -> 0.69 us
  local copies, waits for them, and re-layouts: 10.8 us -> 8.55 us
    unnamed x1 -> x0, blocking collectives: 80 us -> none
    pallas_call x0 -> x1, Pallas kernels: none -> 74.2 us  [shards(): pl.pallas_call(functools.partial(kernel, n_width), out_shape=[VMEM((colum...]
    psum x2 -> x0, blocking collectives: 19.7 us -> none  [one_axis_at_a_time(): array = lax.psum(array, axis)]
    all_gather x1 -> x0, waiting for transfers between devices: 17.4 us -> none  [side_by_side(): result, at, done = (lax.all_gather(both, axis, axis=dim, tiled=True), 0, [])]
    slice x1 -> x0, local copies, waits for them, and re-layouts: 10.5 us -> none  [side_by_side(): done.append(lax.slice_in_dim(result, at, at + a.shape[along], axis=along))]
    unnamed x14 -> x7, local copies, waits for them, and re-layouts: 0.29 us -> 8.47 us
    reduce_sum x1 -> x0, other arithmetic: 2.53 us -> none  [shards(): jnp.sum(whole_up * whole_up, axis=0)]
  transfers between devices with their start and end apart: 1 -> 0, of which waited for: 1 -> 0; matrix products, arithmetic and copies ran while one was open for 0% -> 0% of each run, Pallas kernels for 0% -> 0%
where the time goes in v1:
time: 84.4 us; the launch traced here: 84.1 us
  Pallas kernels  74.2 us (88%)
  local copies, waits for them, and re-layouts  8.55 us (10%)
    pallas_call x1, Pallas kernels, shards(): pl.pallas_call(functools.partial(kernel, n_width), out_shape=[VMEM((colum...  74.2 us
    unnamed x7, local copies, waits for them, and re-layouts  8.47 us

profile of v1, /device:TPU:2, one launch (start us, length us, event | category | flops | bytes accessed | tf_op | source)
XLA Modules:
  0.0 84.1 jit_solution(6601548311795922317)
XLA Ops:
  0.7 0.7 add.18
  1.3 0.1 reshape_tile.3
  1.4 74.2 %shard_map.135 = (bf16[688,4096]{1,0:T(8,128)(2,1)S(1)}, bf16[688,4096]{1,0:T(8,128)(2,1)S(1)}, f32[8,128]{1,0:T(8,128)S(1)}, f32[8,128]{1,0:T(8,128)S(1)}, bf16...) custom-call(f32[688,256]{1,0:T(8,128)} %bitcast.22, f32[688,256]{1,0:T(8,128)} %bitcast.23, ...), custom_call_target="tpu_custom_call" | custom-call | tf_op jit(solution)/shard_map/pallas_call | solution.py:192
  75.6 2.5 %copy.22 = bf16[4096,688]{0,1:T(8,128)(2,1)} copy(bf16[4096,688]{0,1:T(8,128)(2,1)S(1)} %bitcast.16) | data formatting | bytes 11272192
  78.1 2.5 %copy.23 = bf16[4096,688]{0,1:T(8,128)(2,1)} copy(bf16[4096,688]{0,1:T(8,128)(2,1)S(1)} %bitcast.15) | data formatting | bytes 11272192
  80.6 0.6 copy.24
  81.2 0.9 %copy.25 = f32[256,688]{0,1:T(8,128)} copy(f32[256,688]{0,1:T(8,128)S(1)} %bitcast.18) | data formatting | bytes 1409024
  82.0 0.9 %copy.26 = f32[256,688]{0,1:T(8,128)} copy(f32[256,688]{0,1:T(8,128)S(1)} %bitcast.17) | data formatting | bytes 1409024
  82.9 0.6 copy.27
  83.5 0.6 copy.28
  (2 shorter events, 0.0 us)

commit v2 on v1

--- a/solution.py
+++ b/solution.py
@@ -22,10 +22,11 @@
     return [(at, min(LANES, columns - at)) for at in range(0, columns, LANES)]
 
 
-def kernel(n_width, tg, dg, sg, tu, du, su, norm,
+def kernel(n_width, tg, dg, sg, tu, du, su, norm_old, norm_new,
            og, ou, scale_g, scale_u, serve, wg, wu,
-           held, sums, parts, ordered,
-           in_sems, sum_send, sum_recv, part_send, part_recv, send_sems, recv_sems):
+           held, norms, sums, parts, ordered,
+           in_sems, norm_sems, sum_send, sum_recv, part_send, part_recv, serve_send, serve_recv,
+           send_sems, recv_sems, ready):
     y, x, w = lax.axis_index("fsdp_0"), lax.axis_index("fsdp_1"), lax.axis_index("width")
     me = y * RING + x
     columns, rows = wg.shape
@@ -33,9 +34,11 @@
     def at(yy, xx, ww):
         return {"device_id": (yy, xx, ww), "device_id_type": pl.DeviceIdType.MESH}
 
+    norm_loads = [pltpu.make_async_copy(ref, norms.at[i], norm_sems.at[i])
+                  for i, ref in enumerate((norm_old, norm_new))]
     loads = [pltpu.make_async_copy(ref, held.at[i], in_sems.at[i])
              for i, ref in enumerate((tg, dg, sg, tu, du, su))]
-    for load in loads:
+    for load in loads + norm_loads:
         load.start()
 
     plane = sorted(((dy, dx) for dy in range(RING) for dx in range(RING) if dy or dx),
@@ -43,12 +46,28 @@
     mates = [((y + dy) % RING, (x + dx) % RING, w) for dy, dx in plane]
     stack = [(y, x, (w + dw) % n_width) for dw in range(1, n_width)]
 
+    gateway, herald = me == 0, me == 1
     barrier = pltpu.get_barrier_semaphore()
-    for peer in mates + stack:
-        pl.semaphore_signal(barrier, 1, **at(*peer))
+    for peer in mates:
+        @pl.when(peer[0] * RING + peer[1] != 0)
+        def _():
+            pl.semaphore_signal(barrier, 1, **at(*peer))
+
+    @pl.when(gateway)
+    def _():
+        for peer in stack:
+            pl.semaphore_signal(barrier, 1, **at(*peer))
 
     sums[me] = jnp.zeros((16, LANES), jnp.float32)
-    sums[me, NORM_ROW:NORM_ROW + 1, :] = norm[...]
+    for load in norm_loads:
+        load.wait()
+    gain = norms[0] + norms[1]
+    length = gain.shape[1]
+    lane = lax.broadcasted_iota(jnp.int32, (1, LANES), 1)
+    spread = jnp.zeros((1, LANES), jnp.float32)
+    for i in range(length):
+        spread = jnp.where(lane == w * length % LANES + i, gain[:, i:i + 1], spread)
+    sums[me, NORM_ROW:NORM_ROW + 1, :] = spread
     for a, whole in enumerate((wg, wu)):
         for load in loads[3 * a:3 * a + 3]:
             load.wait()
@@ -65,7 +84,17 @@
                 folded = jnp.concatenate([folded, jnp.zeros((LANES - size, LANES), jnp.float32)], axis=0)
             sums[me, 8 * a + k:8 * a + k + 1, :] = jnp.sum(folded.T, axis=0, keepdims=True)
 
-    pl.semaphore_wait(barrier, len(mates) + len(stack))
+    @pl.when(jnp.logical_not(gateway))
+    def _():
+        pl.semaphore_wait(barrier, len(mates))
+
+    @pl.when(herald)
+    def _():
+        pl.semaphore_signal(ready, 1, **at(0, 0, w))
+
+    @pl.when(gateway)
+    def _():
+        pl.semaphore_wait(ready, 1)
 
     sent = []
     for i, peer in enumerate(mates):
@@ -89,8 +118,11 @@
             out[part, own] = (whole[part, :] * factor).astype(jnp.bfloat16)
     scale_g[...] = scale[:8]
     scale_u[...] = scale[8:]
-    for i in range(RING * RING):
-        parts[w, i:i + 1, :] = sums[i, NORM_ROW:NORM_ROW + 1, :]
+
+    @pl.when(gateway)
+    def _():
+        for i in range(RING * RING):
+            parts[w, i:i + 1, :] = sums[i, NORM_ROW:NORM_ROW + 1, :]
 
     half = columns // 2 // 8 * 8
     halves = {1: pl.ds(0, half), -1: pl.ds(half, columns - half)}
@@ -130,10 +162,6 @@
     for a, d in both:
         p, q = spots[a]
         send(("second", a, 0, d), a, 2, d, full, block(a, p, q))
-    for i, mate in enumerate(stack):
-        copy = pltpu.make_async_remote_copy(parts.at[w], parts.at[w], part_send.at[i], part_recv.at[i], **at(*mate))
-        copy.start()
-        sent.append(copy)
     for a, d in both:
         p, q = spots[a]
         receive(("first", a, d), a, 1, d, full, block(a, p - d, q))
@@ -147,6 +175,31 @@
         receive(("pass", a, e), a, 1, e, halves[e], block(a, p - 2 * e, q))
         for d in (1, -1):
             send(("second", a, 2 * e, d), a, 2, d, halves[e], block(a, p + 2, q))
+
+    def part_copy(i, slot):
+        return pltpu.make_async_remote_copy(parts.at[slot], parts.at[slot], part_send.at[i], part_recv.at[i],
+                                            **at(*stack[i]))
+
+    def serve_copy(i, peer):
+        return pltpu.make_async_remote_copy(serve, serve, serve_send.at[i], serve_recv, **at(*peer))
+
+    @pl.when(gateway)
+    def _():
+        pl.semaphore_wait(barrier, len(stack))
+        for i in range(len(stack)):
+            part_copy(i, w).start()
+        for i in range(len(stack)):
+            part_copy(i, (w + n_width - (i + 1)) % n_width).wait_recv()
+        strips = ordered.shape[0] // 16
+        for b in range(strips):
+            group = [parts[i] for i in range(b * n_width // strips, (b + 1) * n_width // strips)]
+            ordered[pl.ds(b, 16, stride=strips), :] = functools.reduce(jnp.add, group)
+        serve[...] = ordered[...].astype(jnp.bfloat16)
+        for i in range(len(stack)):
+            part_copy(i, w).wait_send()
+        for i, peer in enumerate(mates):
+            serve_copy(i, peer).start()
+
     for e in (0, 1, -1):
         for a, d in both:
             p, q = spots[a]
@@ -156,16 +209,6 @@
         p, q = spots[a]
         receive(("second", a, 2 * d, d), a, 2, d, halves[d], block(a, p + 2, q - d))
         send(("end", a, 2, d), a, 2, d, halves[d], block(a, p + 2, q - d))
-
-    for i, (_, _, target) in enumerate(stack):
-        source = (w + n_width - (i + 1)) % n_width
-        pltpu.make_async_remote_copy(parts.at[source], parts.at[source], part_send.at[i], part_recv.at[i],
-                                     **at(*stack[i])).wait_recv()
-    strips = ordered.shape[0] // 16
-    for b in range(strips):
-        group = [parts[i] for i in range(b * n_width // strips, (b + 1) * n_width // strips)]
-        ordered[pl.ds(b, 16, stride=strips), :] = functools.reduce(jnp.add, group)
-    serve[...] = ordered[...].astype(jnp.bfloat16)
 
     for a, d in both:
         p, q = spots[a]
@@ -177,19 +220,41 @@
     for copy in sent:
         copy.wait_send()
 
+    @pl.when(gateway)
+    def _():
+        for i, peer in enumerate(mates):
+            serve_copy(i, peer).wait_send()
+
+    @pl.when(jnp.logical_not(gateway))
+    def _():
+        serve_copy(0, mates[0]).wait_recv()
+
+
+def flush(*refs):
+    n = len(refs) // 2
+    sources, targets, sems = refs[:n], refs[n:2 * n], refs[2 * n]
+    copies = []
+    for source, target in zip(sources, targets):
+        rows = source.shape[0]
+        pieces = 4 if rows >= LANES else 1
+        size = -(-rows // pieces // 16) * 16
+        for start in range(0, rows, size):
+            part = pl.ds(start, min(size, rows - start))
+            copies.append(pltpu.make_async_copy(source.at[part], target.at[part], sems.at[len(copies)]))
+    for copy in copies:
+        copy.start()
+    for copy in copies:
+        copy.wait()
+
 
 def shards(n_width, train_gate, drift_gate, spread_gate, train_up, drift_up, spread_up, norm_train, norm_step):
     rows, columns = train_gate.shape
     length = norm_train.shape[0]
     strips = n_width * length // LANES
-    slot = lax.axis_index("width") * length % LANES // length
-    lane = lax.broadcasted_iota(jnp.int32, (1, LANES), 1) // length
-    norm = jnp.tile(norm_train + norm_step, LANES // length).reshape(1, LANES)
-    norm = jnp.where(lane == slot, norm, 0.0)
     n_copies = 2 * 22
     VMEM, DMA = pltpu.VMEM, pltpu.SemaphoreType.DMA
     space = pl.BlockSpec(memory_space=pltpu.VMEM)
-    og, ou, scale_g, scale_u, serve, wg, wu = pl.pallas_call(
+    on_chip = pl.pallas_call(
         functools.partial(kernel, n_width),
         out_shape=[
             VMEM((columns, RING * RING * rows), jnp.bfloat16),
@@ -200,24 +265,38 @@
             VMEM((columns, rows), jnp.float32),
             VMEM((columns, rows), jnp.float32),
         ],
-        in_specs=[pl.BlockSpec(memory_space=pltpu.HBM)] * 6 + [space],
+        in_specs=[pl.BlockSpec(memory_space=pltpu.HBM)] * 8,
         out_specs=[space] * 7,
         scratch_shapes=[
             VMEM((6, columns, rows), jnp.float32),
+            VMEM((2, 1, length), jnp.float32),
             VMEM((RING * RING, 16, LANES), jnp.float32),
             VMEM((n_width, 16, LANES), jnp.float32),
             VMEM((16 * strips, LANES), jnp.float32),
             DMA((6,)),
+            DMA((2,)),
             DMA((RING * RING - 1,)),
             DMA((RING * RING - 1,)),
             DMA((n_width - 1,)),
             DMA((n_width - 1,)),
+            DMA((RING * RING - 1,)),
+            DMA(()),
             DMA((n_copies,)),
             DMA((n_copies,)),
+            pltpu.SemaphoreType.REGULAR,
         ],
         compiler_params=pltpu.CompilerParams(collective_id=0, has_side_effects=True, vmem_limit_bytes=32 * 2**20),
-    )(*(pltpu.with_memory_space_constraint(a.T, pltpu.HBM)
-        for a in (train_gate, drift_gate, spread_gate, train_up, drift_up, spread_up)), norm)
+    )(*(pltpu.with_memory_space_constraint(a, pltpu.HBM) for a in (
+        train_gate.T, drift_gate.T, spread_gate.T, train_up.T, drift_up.T, spread_up.T,
+        norm_train.reshape(1, length), norm_step.reshape(1, length))))
+    og, ou, scale_g, scale_u, serve, wg, wu = pl.pallas_call(
+        flush,
+        out_shape=[pltpu.HBM(a.shape, a.dtype) for a in on_chip],
+        in_specs=[space] * 7,
+        out_specs=[pl.BlockSpec(memory_space=pltpu.HBM)] * 7,
+        scratch_shapes=[DMA((19,))],
+        compiler_params=pltpu.CompilerParams(vmem_limit_bytes=2**20),
+    )(*(pltpu.with_memory_space_constraint(a, pltpu.VMEM) for a in on_chip))
     return (
         og.T, ou.T, scale_g.reshape(-1)[:columns], scale_u.reshape(-1)[:columns],
         serve.reshape(-1), wg.T, wu.T,

time: 84.4 us -> 76.1 us (0.902)
  local copies, waits for them, and re-layouts: 8.55 us -> 0 us
  Pallas kernels: 74.2 us -> 75.4 us
    unnamed x7 -> x0, local copies, waits for them, and re-layouts: 8.47 us -> none
    pallas_call x0 -> x1, Pallas kernels: none -> 4.73 us  [shards(): pl.pallas_call(flush, out_shape=[pltpu.HBM(a.shape, a.dtype) for a in on_...]
    pallas_call x1, Pallas kernels: 74.2 us -> 70.6 us  [shards(): pl.pallas_call(functools.partial(kernel, n_width), out_shape=[VMEM((colum...]
where the time goes in v2:
time: 76.1 us; the launch traced here: 76 us
  Pallas kernels  75.4 us (99%)
    pallas_call x1, Pallas kernels, shards(): pl.pallas_call(functools.partial(kernel, n_width), out_shape=[VMEM((colum...  70.6 us
    pallas_call x1, Pallas kernels, shards(): pl.pallas_call(flush, out_shape=[pltpu.HBM(a.shape, a.dtype) for a in on_...  4.73 us

profile of v2, /device:TPU:2, one launch (start us, length us, event | category | flops | bytes accessed | tf_op | source)
XLA Modules:
  0.0 76.0 jit_solution(5589502200049641712)
XLA Ops:
  0.6 70.6 %shard_map.135 = (bf16[688,4096]{1,0:T(8,128)(2,1)S(1)}, bf16[688,4096]{1,0:T(8,128)(2,1)S(1)}, f32[8,128]{1,0:T(8,128)S(1)}, f32[8,128]{1,0:T(8,128)S(1)}, bf16...) custom-call(f32[688,256]{1,0:T(8,128)} %bitcast.17, f32[688,256]{1,0:T(8,128)} %bitcast.18, ...), custom_call_target="tpu_custom_call" | custom-call | tf_op jit(solution)/shard_map/pallas_call | solution.py:257
  71.3 4.7 %shard_map.136 = (bf16[688,4096]{1,0:T(8,128)(2,1)}, bf16[688,4096]{1,0:T(8,128)(2,1)}, f32[8,128]{1,0:T(8,128)}, f32[8,128]{1,0:T(8,128)}, bf16[32,128]{1,0:T(8...) custom-call(bf16[688,4096]{1,0:T(8,128)(2,1)S(1)} %get-tuple-element.21.refs_0_, ...), custom_call_target="tpu_custom_call" | custom-call | tf_op jit(solution)/shard_map/pallas_call | solution.py:292

commit v3 on v2

--- a/solution.py
+++ b/solution.py
@@ -13,6 +13,7 @@
 RING = 4
 LANES = 128
 NORM_ROW = 14
+EARLY = 112
 
 learn_rate = 0.3
 hold_rate = 0.9
@@ -22,9 +23,9 @@
     return [(at, min(LANES, columns - at)) for at in range(0, columns, LANES)]
 
 
-def kernel(n_width, tg, dg, sg, tu, du, su, norm_old, norm_new,
+def kernel(n_width, early, tg, dg, sg, tu, du, su, norm_old, norm_new,
            og, ou, scale_g, scale_u, serve, wg, wu,
-           held, norms, sums, parts, ordered,
+           held, raw, norms, sums, parts, ordered,
            in_sems, norm_sems, sum_send, sum_recv, part_send, part_recv, serve_send, serve_recv,
            send_sems, recv_sems, ready):
     y, x, w = lax.axis_index("fsdp_0"), lax.axis_index("fsdp_1"), lax.axis_index("width")
@@ -96,9 +97,51 @@
     def _():
         pl.semaphore_wait(ready, 1)
 
+    half = columns // 2 // 8 * 8
+    halves = {1: pl.ds(0, half), -1: pl.ds(half, columns - half)}
+    full, late = pl.ds(0, columns), pl.ds(early, columns - early)
+    outs = (og, ou)
+    keys = {}
+
+    def block(a, p, q):
+        p, q = (p + RING) % RING, (q + RING) % RING
+        index = q * RING + p if a == 0 else p * RING + q
+        return pl.ds(pl.multiple_of(index * rows, LANES), rows)
+
+    def peer(a, phase, d):
+        along_x = (a == 0) == (phase == 1)
+        if along_x:
+            return at(y, (x + d + RING) % RING, w)
+        return at((y + d + RING) % RING, x, w)
+
+    def copy_of(key, a, phase, d, part, cols):
+        index = keys.setdefault(key, len(keys))
+        ref = outs[a].at[part, cols]
+        return pltpu.make_async_remote_copy(ref, ref, send_sems.at[index], recv_sems.at[index], **peer(a, phase, d))
+
+    def send(key, a, phase, d, part, cols):
+        copy = copy_of(key, a, phase, d, part, cols)
+        copy.start()
+        sent.append(copy)
+
+    def receive(key, a, phase, d, part, cols):
+        copy_of(key, a, phase, d, part, cols).wait_recv()
+
+    spots = ((x, y), (y, x))
+    both = [(a, d) for a in range(2) for d in (1, -1)]
     sent = []
-    for i, peer in enumerate(mates):
-        copy = pltpu.make_async_remote_copy(sums.at[me], sums.at[me], sum_send.at[i], sum_recv.at[i], **at(*peer))
+    for i, mate in enumerate(mates):
+        copy = pltpu.make_async_remote_copy(sums.at[me], sums.at[me], sum_send.at[i], sum_recv.at[i], **at(*mate))
+        copy.start()
+        sent.append(copy)
+
+    def raw_copy(a, d):
+        index = keys.setdefault(("raw", a, d), len(keys))
+        return pltpu.make_async_remote_copy((wg, wu)[a].at[pl.ds(0, early)], raw.at[a, (1 - d) // 2],
+                                            send_sems.at[index], recv_sems.at[index], **peer(a, 1, d))
+
+    for a, d in both:
+        copy = raw_copy(a, d)
         copy.start()
         sent.append(copy)
     for i, (dy, dx) in enumerate(plane):
@@ -110,12 +153,15 @@
         total = total + sums[i]
     scale = jnp.sqrt(total)
     inverse = jnp.concatenate([1.0 / scale, jnp.zeros((LANES - 16, LANES), jnp.float32)], axis=0).T
-    own = pl.ds(pl.multiple_of(me * rows, LANES), rows)
-    for a, (whole, out) in enumerate(((wg, og), (wu, ou))):
-        for k, (start, size) in enumerate(chunks(columns)):
+
+    def scaled(a, source, count, cols):
+        for k, (start, size) in enumerate(chunks(count)):
             part = pl.ds(start, size)
             factor = inverse[:size, 8 * a + k:8 * a + k + 1]
-            out[part, own] = (whole[part, :] * factor).astype(jnp.bfloat16)
+            outs[a][part, cols] = (source[part, :] * factor).astype(jnp.bfloat16)
+
+    for a, whole in enumerate((wg, wu)):
+        scaled(a, whole, columns, pl.ds(pl.multiple_of(me * rows, LANES), rows))
     scale_g[...] = scale[:8]
     scale_u[...] = scale[8:]
 
@@ -124,47 +170,19 @@
         for i in range(RING * RING):
             parts[w, i:i + 1, :] = sums[i, NORM_ROW:NORM_ROW + 1, :]
 
-    half = columns // 2 // 8 * 8
-    halves = {1: pl.ds(0, half), -1: pl.ds(half, columns - half)}
-    full = pl.ds(0, columns)
-    outs = (og, ou)
-    keys = {}
-
-    def block(a, p, q):
-        p, q = (p + RING) % RING, (q + RING) % RING
-        index = q * RING + p if a == 0 else p * RING + q
-        return pl.ds(pl.multiple_of(index * rows, LANES), rows)
-
-    def peer(a, phase, d):
-        along_x = (a == 0) == (phase == 1)
-        if along_x:
-            return at(y, (x + d + RING) % RING, w)
-        return at((y + d + RING) % RING, x, w)
-
-    def copy_of(key, a, phase, d, part, cols):
-        index = keys.setdefault(key, len(keys))
-        ref = outs[a].at[part, cols]
-        return pltpu.make_async_remote_copy(ref, ref, send_sems.at[index], recv_sems.at[index], **peer(a, phase, d))
-
-    def send(key, a, phase, d, part, cols):
-        copy = copy_of(key, a, phase, d, part, cols)
-        copy.start()
-        sent.append(copy)
-
-    def receive(key, a, phase, d, part, cols):
-        copy_of(key, a, phase, d, part, cols).wait_recv()
-
-    spots = ((x, y), (y, x))
-    both = [(a, d) for a in range(2) for d in (1, -1)]
-    for a, d in both:
-        p, q = spots[a]
-        send(("first", a, d), a, 1, d, full, block(a, p, q))
+    for a, d in both:
+        p, q = spots[a]
+        send(("first", a, d), a, 1, d, late, block(a, p, q))
     for a, d in both:
         p, q = spots[a]
         send(("second", a, 0, d), a, 2, d, full, block(a, p, q))
     for a, d in both:
         p, q = spots[a]
-        receive(("first", a, d), a, 1, d, full, block(a, p - d, q))
+        raw_copy(a, d).wait_recv()
+        scaled(a, raw.at[a, (1 - d) // 2], early, block(a, p - d, q))
+    for a, d in both:
+        p, q = spots[a]
+        receive(("first", a, d), a, 1, d, late, block(a, p - d, q))
         send(("pass", a, d), a, 1, d, halves[d], block(a, p - d, q))
     for a, e in both:
         p, q = spots[a]
@@ -251,11 +269,12 @@
     rows, columns = train_gate.shape
     length = norm_train.shape[0]
     strips = n_width * length // LANES
-    n_copies = 2 * 22
+    n_copies = 2 * 24
+    early = min(EARLY, columns // 16 * 8)
     VMEM, DMA = pltpu.VMEM, pltpu.SemaphoreType.DMA
     space = pl.BlockSpec(memory_space=pltpu.VMEM)
     on_chip = pl.pallas_call(
-        functools.partial(kernel, n_width),
+        functools.partial(kernel, n_width, early),
         out_shape=[
             VMEM((columns, RING * RING * rows), jnp.bfloat16),
             VMEM((columns, RING * RING * rows), jnp.bfloat16),
@@ -269,6 +288,7 @@
         out_specs=[space] * 7,
         scratch_shapes=[
             VMEM((6, columns, rows), jnp.float32),
+            VMEM((2, 2, early, rows), jnp.float32),
             VMEM((2, 1, length), jnp.float32),
             VMEM((RING * RING, 16, LANES), jnp.float32),
             VMEM((n_width, 16, LANES), jnp.float32),

time: 76.1 us -> 75 us (0.986)
  Pallas kernels: 75.4 us -> 74.2 us
    pallas_call x1, Pallas kernels: 70.6 us -> 69.5 us  [shards(): pl.pallas_call(functools.partial(kernel, n_width, early), out_shape=[VMEM...]
where the time goes in v3:
time: 75 us; the launch traced here: 74.9 us
  Pallas kernels  74.2 us (99%)
    pallas_call x1, Pallas kernels, shards(): pl.pallas_call(functools.partial(kernel, n_width, early), out_shape=[VMEM...  69.5 us
    pallas_call x1, Pallas kernels, shards(): pl.pallas_call(flush, out_shape=[pltpu.HBM(a.shape, a.dtype) for a in on_...  4.73 us

profile of v3, /device:TPU:2, one launch (start us, length us, event | category | flops | bytes accessed | tf_op | source)
XLA Modules:
  0.0 74.9 jit_solution(17312860472422176801)
XLA Ops:
  0.6 69.5 %shard_map.135 = (bf16[688,4096]{1,0:T(8,128)(2,1)S(1)}, bf16[688,4096]{1,0:T(8,128)(2,1)S(1)}, f32[8,128]{1,0:T(8,128)S(1)}, f32[8,128]{1,0:T(8,128)S(1)}, bf16...) custom-call(f32[688,256]{1,0:T(8,128)} %bitcast.17, f32[688,256]{1,0:T(8,128)} %bitcast.18, ...), custom_call_target="tpu_custom_call" | custom-call | tf_op jit(solution)/shard_map/pallas_call | solution.py:276
  70.2 4.7 %shard_map.136 = (bf16[688,4096]{1,0:T(8,128)(2,1)}, bf16[688,4096]{1,0:T(8,128)(2,1)}, f32[8,128]{1,0:T(8,128)}, f32[8,128]{1,0:T(8,128)}, bf16[32,128]{1,0:T(8...) custom-call(bf16[688,4096]{1,0:T(8,128)(2,1)S(1)} %get-tuple-element.21.refs_0_, ...), custom_call_target="tpu_custom_call" | custom-call | tf_op jit(solution)/shard_map/pallas_call | solution.py:312

commit v4 on v3

--- a/solution.py
+++ b/solution.py
@@ -12,8 +12,8 @@
 FSDP_WIDTH = ("fsdp_0", "fsdp_1", "width")
 RING = 4
 LANES = 128
-NORM_ROW = 14
-EARLY = 112
+HALF_ROWS = 6
+EARLY = 128
 
 learn_rate = 0.3
 hold_rate = 0.9
@@ -59,7 +59,7 @@
         for peer in stack:
             pl.semaphore_signal(barrier, 1, **at(*peer))
 
-    sums[me] = jnp.zeros((16, LANES), jnp.float32)
+    sums[me] = jnp.zeros((2 * HALF_ROWS, LANES), jnp.float32)
     for load in norm_loads:
         load.wait()
     gain = norms[0] + norms[1]
@@ -67,8 +67,8 @@
     lane = lax.broadcasted_iota(jnp.int32, (1, LANES), 1)
     spread = jnp.zeros((1, LANES), jnp.float32)
     for i in range(length):
-        spread = jnp.where(lane == w * length % LANES + i, gain[:, i:i + 1], spread)
-    sums[me, NORM_ROW:NORM_ROW + 1, :] = spread
+        spread = jnp.where(lane == LANES - length + i, gain[:, i:i + 1], spread)
+    sums[me, HALF_ROWS - 1:HALF_ROWS, :] = spread
     for a, whole in enumerate((wg, wu)):
         for load in loads[3 * a:3 * a + 3]:
             load.wait()
@@ -83,7 +83,9 @@
                 folded = folded + square[:, j:j + LANES]
             if size < LANES:
                 folded = jnp.concatenate([folded, jnp.zeros((LANES - size, LANES), jnp.float32)], axis=0)
-            sums[me, 8 * a + k:8 * a + k + 1, :] = jnp.sum(folded.T, axis=0, keepdims=True)
+            line = jnp.sum(folded.T, axis=0, keepdims=True)
+            row = HALF_ROWS * a + k
+            sums[me, row:row + 1, :] = line + spread if row == HALF_ROWS - 1 else line
 
     @pl.when(jnp.logical_not(gateway))
     def _():
@@ -152,34 +154,44 @@
     for i in range(1, RING * RING):
         total = total + sums[i]
     scale = jnp.sqrt(total)
-    inverse = jnp.concatenate([1.0 / scale, jnp.zeros((LANES - 16, LANES), jnp.float32)], axis=0).T
+    inverse = jnp.concatenate([1.0 / scale, jnp.zeros((LANES - 2 * HALF_ROWS, LANES), jnp.float32)], axis=0).T
 
     def scaled(a, source, count, cols):
         for k, (start, size) in enumerate(chunks(count)):
             part = pl.ds(start, size)
-            factor = inverse[:size, 8 * a + k:8 * a + k + 1]
+            factor = inverse[:size, HALF_ROWS * a + k:HALF_ROWS * a + k + 1]
             outs[a][part, cols] = (source[part, :] * factor).astype(jnp.bfloat16)
 
     for a, whole in enumerate((wg, wu)):
         scaled(a, whole, columns, pl.ds(pl.multiple_of(me * rows, LANES), rows))
-    scale_g[...] = scale[:8]
-    scale_u[...] = scale[8:]
+    for a, out in enumerate((scale_g, scale_u)):
+        out[...] = jnp.zeros_like(out)
+        out[:HALF_ROWS, :] = scale[HALF_ROWS * a:HALF_ROWS * (a + 1)]
 
     @pl.when(gateway)
     def _():
         for i in range(RING * RING):
-            parts[w, i:i + 1, :] = sums[i, NORM_ROW:NORM_ROW + 1, :]
-
+            parts[w, i:i + 1, :] = sums[i, HALF_ROWS - 1:HALF_ROWS, :]
+        gains, placed = parts[w], jnp.zeros((16, LANES), jnp.float32)
+        for i in range(length):
+            placed = jnp.where(lane == w * length % LANES + i, gains[:, LANES - length + i:LANES - length + i + 1], placed)
+        parts[w] = placed
+
+    def land_raw():
+        for a, d in both:
+            p, q = spots[a]
+            raw_copy(a, d).wait_recv()
+            scaled(a, raw.at[a, (1 - d) // 2], early, block(a, p - d, q))
+
+    first_core = w % 2 == 0
+    pl.when(first_core)(land_raw)
     for a, d in both:
         p, q = spots[a]
         send(("first", a, d), a, 1, d, late, block(a, p, q))
     for a, d in both:
         p, q = spots[a]
         send(("second", a, 0, d), a, 2, d, full, block(a, p, q))
-    for a, d in both:
-        p, q = spots[a]
-        raw_copy(a, d).wait_recv()
-        scaled(a, raw.at[a, (1 - d) // 2], early, block(a, p - d, q))
+    pl.when(jnp.logical_not(first_core))(land_raw)
     for a, d in both:
         p, q = spots[a]
         receive(("first", a, d), a, 1, d, late, block(a, p - d, q))
@@ -290,7 +302,7 @@
             VMEM((6, columns, rows), jnp.float32),
             VMEM((2, 2, early, rows), jnp.float32),
             VMEM((2, 1, length), jnp.float32),
-            VMEM((RING * RING, 16, LANES), jnp.float32),
+            VMEM((RING * RING, 2 * HALF_ROWS, LANES), jnp.float32),
             VMEM((n_width, 16, LANES), jnp.float32),
             VMEM((16 * strips, LANES), jnp.float32),
             DMA((6,)),

time: 75 us -> 74.8 us (level)
  no operation moved by 1% of the time
where the time goes in v4:
time: 74.8 us; the launch traced here: 74.7 us
  Pallas kernels  74.1 us (99%)
    pallas_call x1, Pallas kernels, shards(): pl.pallas_call(functools.partial(kernel, n_width, early), out_shape=[VMEM...  69.3 us
    pallas_call x1, Pallas kernels, shards(): pl.pallas_call(flush, out_shape=[pltpu.HBM(a.shape, a.dtype) for a in on_...  4.73 us

profile of v4, /device:TPU:2, one launch (start us, length us, event | category | flops | bytes accessed | tf_op | source)
XLA Modules:
  0.0 74.7 jit_solution(11394450351803022964)
XLA Ops:
  0.6 69.3 %shard_map.135 = (bf16[688,4096]{1,0:T(8,128)(2,1)S(1)}, bf16[688,4096]{1,0:T(8,128)(2,1)S(1)}, f32[8,128]{1,0:T(8,128)S(1)}, f32[8,128]{1,0:T(8,128)S(1)}, bf16...) custom-call(f32[688,256]{1,0:T(8,128)} %bitcast.17, f32[688,256]{1,0:T(8,128)} %bitcast.18, ...), custom_call_target="tpu_custom_call" | custom-call | tf_op jit(solution)/shard_map/pallas_call | solution.py:288
  70.0 4.7 %shard_map.136 = (bf16[688,4096]{1,0:T(8,128)(2,1)}, bf16[688,4096]{1,0:T(8,128)(2,1)}, f32[8,128]{1,0:T(8,128)}, f32[8,128]{1,0:T(8,128)}, bf16[32,128]{1,0:T(8...) custom-call(bf16[688,4096]{1,0:T(8,128)(2,1)S(1)} %get-tuple-element.21.refs_0_, ...), custom_call_target="tpu_custom_call" | custom-call | tf_op jit(solution)/shard_map/pallas_call | solution.py:324
